TPU v7x, 32 devices: a whole 2x2x4 slice. The times are simulated.
32 devices in a mesh: ens: 4 (over y, x), slab: 8 (over z, core).
Axes of the slice: x: 2, y: 2, z: 4, core: 2. Of those that a mesh axis runs over, the one named last changes fastest.
Arguments:
- density0: float32 [192, 1024], P('slab'), may hold values from 0.5 to 1.5
- relax_rate: float32 [192, 1024], P('slab'), may hold values from 0.6 to 1.8
- perturbation: int32 [4, 192, 1024], P('ens', 'slab'), may hold values from -3 to 3
Outputs:
- lifted: float32 [4, 9, 192, 1024], P('ens', None, 'slab')
- projected: float32 [192, 1024], P('slab')
All inputs are finite; a program needn't handle non-finite values.
Results may differ from a plain program's by a relative error of at most 0.0002.
Values sent between devices are 32-bit elements; how exact they have to be, the bound alone decides.
A program may use at most 64 MiB of HBM per device.

v0:
```python
import functools

import jax
import jax.numpy as jnp
from jax import lax
from jax.experimental import pallas as pl
from jax.experimental.pallas import tpu as pltpu
from jax.sharding import PartitionSpec as P

MICRO_SPELLS = 3
STEPS = 8
TOTAL = MICRO_SPELLS * STEPS
LANES = 128
CHUNK = 4

row_moves = (0, 0, 1, 0, -1, 1, 1, -1, -1)
col_moves = (0, 1, 0, -1, 0, 1, -1, -1, 1)
lattice_weights = (4.0 / 9.0,) + (1.0 / 9.0,) * 4 + (1.0 / 36.0,) * 4
shift_amp = 0.08
step_cap = 0.25
MESH = pl.DeviceIdType.MESH


def roll_columns(x, move):
    if move == 0:
        return x
    subs = x.shape[1]
    lane = lax.broadcasted_iota(jnp.int32, x.shape, 2)
    if move == 1:
        within = pltpu.roll(x, 1, 2)
        across = pltpu.roll(within, 1, 1)
        return jnp.where(lane == 0, across, within)
    within = pltpu.roll(x, LANES - 1, 2)
    across = pltpu.roll(within, subs - 1, 1)
    return jnp.where(lane == LANES - 1, across, within)


def collide(f, relax):
    s13, d13 = f[1] + f[3], f[1] - f[3]
    s24, d24 = f[2] + f[4], f[2] - f[4]
    s57, d57 = f[5] + f[7], f[5] - f[7]
    s68, d68 = f[6] + f[8], f[6] - f[8]
    density = (f[0] + (s13 + s24)) + (s57 + s68)
    mom_row = d24 + (d57 + d68)
    mom_col = d13 + (d57 - d68)
    inverse = 1.0 / density
    vel_row = mom_row * inverse
    vel_col = mom_col * inverse
    keep = 1.0 - relax
    third = relax * (1.0 / 3.0)
    third_row = third * mom_row
    third_col = third * mom_col
    half_rr = third_row * vel_row * 1.5
    half_cc = third_col * vel_col * 1.5
    quarter_rc = third_row * vel_col * 0.75
    squares = half_rr + half_cc
    base = (relax * density) * (1.0 / 9.0) - squares * (1.0 / 3.0)
    even_col = base + half_cc
    even_row = base + half_rr
    corner = 0.25 * (base + squares)
    even_57 = corner + quarter_rc
    even_68 = corner - quarter_rc
    odd_57 = 0.25 * (third_row + third_col)
    odd_68 = 0.25 * (third_row - third_col)
    k = [keep * value for value in f]
    return (
        k[0] + 4.0 * base,
        k[1] + (even_col + third_col),
        k[2] + (even_row + third_row),
        k[3] + (even_col - third_col),
        k[4] + (even_row - third_row),
        k[5] + (even_57 + odd_57),
        k[6] + (even_68 + odd_68),
        k[7] + (even_57 - odd_57),
        k[8] + (even_68 - odd_68),
    )


def kernel(
    ens,
    slabs,
    density_hbm,
    relax_hbm,
    pert_hbm,
    finals,
    last_rho,
    change_out,
    fitted_out,
    gain_out,
    density_in,
    relax_in,
    pert_in,
    start,
    relax,
    buf,
    gathered,
    squares,
    load_sem,
    halo_send,
    halo_recv,
    ens_send,
    ens_recv,
    sq_send,
    sq_recv,
):
    height, width = density_in.shape
    subs = width // LANES
    rows = height + 2 * TOTAL
    me_e = lax.axis_index("ens")
    me_s = lax.axis_index("slab")

    barrier = pltpu.get_barrier_semaphore()
    for k in range(1, ens):
        pl.semaphore_signal(
            barrier, inc=1, device_id={"ens": lax.rem(me_e + k, ens)}, device_id_type=MESH
        )
    for k in range(1, slabs):
        pl.semaphore_signal(
            barrier, inc=1, device_id={"slab": lax.rem(me_s + k, slabs)}, device_id_type=MESH
        )

    loads = [
        pltpu.make_async_copy(relax_hbm, relax_in, load_sem.at[0]),
        pltpu.make_async_copy(density_hbm, density_in, load_sem.at[1]),
        pltpu.make_async_copy(pert_hbm.at[0], pert_in, load_sem.at[2]),
    ]
    for load in loads:
        load.start()
    own = pl.ds(TOTAL, height)
    loads[0].wait()
    for s in range(subs):
        relax[own, s, :] = relax_in[:, s * LANES : (s + 1) * LANES]
    loads[1].wait()
    loads[2].wait()
    for s in range(subs):
        cols = slice(s * LANES, (s + 1) * LANES)
        start[own, s, :] = density_in[:, cols] + shift_amp * pert_in[:, cols].astype(jnp.float32)

    pl.semaphore_wait(barrier, ens + slabs - 2)
    right = lax.rem(me_s + 1, slabs)
    left = lax.rem(me_s + slabs - 1, slabs)
    halos = []
    for n, field in enumerate((relax, start)):
        for side, (target, source, dest) in enumerate(
            ((right, height, 0), (left, TOTAL, TOTAL + height))
        ):
            halos.append(
                pltpu.make_async_remote_copy(
                    src_ref=field.at[pl.ds(source, TOTAL)],
                    dst_ref=field.at[pl.ds(dest, TOTAL)],
                    send_sem=halo_send.at[n, side],
                    recv_sem=halo_recv.at[n, side],
                    device_id={"slab": target},
                    device_id_type=MESH,
                )
            )
    for copy in halos:
        copy.start()

    def first_rows(low, high):
        def body(c, carry):
            at = pl.ds(low + c * CHUNK, CHUNK)
            fresh = start[at]
            out = collide([weight * fresh for weight in lattice_weights], relax[at])
            for i in range(9):
                buf[1, i, at] = roll_columns(out[i], col_moves[i])
            return carry

        lax.fori_loop(0, (high - low) // CHUNK, body, 0)

    def step(k, carry):
        source, dest = lax.rem(k + 1, 2), lax.rem(k, 2)

        def body(c, inner):
            at = k - 1 + c * CHUNK
            f = [buf[source, i, pl.ds(at - row_moves[i], CHUNK)] for i in range(9)]
            out = collide(f, relax[pl.ds(at, CHUNK)])
            for i in range(9):
                buf[dest, i, pl.ds(at, CHUNK)] = roll_columns(out[i], col_moves[i])
            return inner

        lax.fori_loop(0, (rows - 2 * k + 2 + CHUNK - 1) // CHUNK, body, 0)
        return carry

    def spell_density(spell, parity):
        def body(c, inner):
            at = TOTAL + c * CHUNK
            total = buf[parity, 0, pl.ds(at, CHUNK)]
            for i in range(1, 9):
                total = total + buf[parity, i, pl.ds(at - row_moves[i], CHUNK)]
            gathered[spell, me_e, pl.ds(c * CHUNK, CHUNK)] = total
            return inner

        lax.fori_loop(0, height // CHUNK, body, 0)
        copies = []
        for k in range(1, ens):
            copies.append(
                pltpu.make_async_remote_copy(
                    src_ref=gathered.at[spell, me_e],
                    dst_ref=gathered.at[spell, me_e],
                    send_sem=ens_send.at[spell, k - 1],
                    recv_sem=ens_recv.at[spell, k - 1],
                    device_id={"ens": lax.rem(me_e + k, ens)},
                    device_id_type=MESH,
                )
            )
        for copy in copies:
            copy.start()
        return copies

    first_rows(TOTAL, TOTAL + height)
    for copy in halos:
        copy.wait_recv()
    first_rows(0, TOTAL)
    first_rows(TOTAL + height, rows)

    sent = []
    for spell in range(MICRO_SPELLS):
        lax.fori_loop(max(2, spell * STEPS + 1), (spell + 1) * STEPS + 1, step, 0)
        sent.append(spell_density(spell, ((spell + 1) * STEPS) % 2))

    parity = TOTAL % 2
    for s in range(subs):
        cols = slice(s * LANES, (s + 1) * LANES)
        for i in range(9):
            finals[i, :, cols] = buf[parity, i, pl.ds(TOTAL - row_moves[i], height), s, :]
        last_rho[:, cols] = gathered[MICRO_SPELLS - 1, me_e, :, s, :]

    for copies in sent:
        for copy in copies:
            copy.wait_recv()

    def mean(spell, at):
        total = gathered[spell, 0, at]
        for member in range(1, ens):
            total = total + gathered[spell, member, at]
        return total * (1.0 / ens)

    def fit(c, acc):
        at = pl.ds(c * CHUNK, CHUNK)
        first, middle, last = (mean(spell, at) for spell in range(MICRO_SPELLS))
        change = last - first
        start[at] = change
        relax[at] = (first + middle + last) * (1.0 / 3.0) + 0.5 * change
        return acc + jnp.sum(change * change, axis=0)

    acc = lax.fori_loop(0, height // CHUNK, fit, jnp.zeros((subs, LANES), jnp.float32))
    squares[me_s] = acc
    copies = []
    for k in range(1, slabs):
        copies.append(
            pltpu.make_async_remote_copy(
                src_ref=squares.at[me_s],
                dst_ref=squares.at[me_s],
                send_sem=sq_send.at[k - 1],
                recv_sem=sq_recv.at[k - 1],
                device_id={"slab": lax.rem(me_s + k, slabs)},
                device_id_type=MESH,
            )
        )
    for copy in copies:
        copy.start()
    for s in range(subs):
        cols = slice(s * LANES, (s + 1) * LANES)
        change_out[:, cols] = start[pl.ds(0, height), s, :]
        fitted_out[:, cols] = relax[pl.ds(0, height), s, :]
    for copy in copies:
        copy.wait_recv()
    total = jnp.sum(jnp.sum(squares[...], axis=0), axis=(0, 1), keepdims=True)
    mean_square = total * (1.0 / (height * width * slabs))
    gain = step_cap / jnp.sqrt(mean_square + 1e-06)
    gain_out[...] = jnp.broadcast_to(gain, gain_out.shape)

    for group in [halos, copies] + sent:
        for copy in group:
            copy.wait_send()


def on_device(density0, relax_rate, perturbation):
    height, width = density0.shape
    ens, slabs = lax.axis_size("ens"), lax.axis_size("slab")
    assert perturbation.shape[0] == 1 and height >= TOTAL and width % LANES == 0
    assert height % CHUNK == 0 and TOTAL % CHUNK == 0
    subs = width // LANES
    rows = height + 2 * TOTAL + CHUNK
    f32 = jnp.float32
    field = jax.ShapeDtypeStruct((height, width), f32)
    vmem = pl.BlockSpec(memory_space=pltpu.VMEM)
    dma = pltpu.SemaphoreType.DMA
    finals, last_rho, change, fitted, gain = pl.pallas_call(
        functools.partial(kernel, ens, slabs),
        out_shape=(
            jax.ShapeDtypeStruct((9, height, width), f32),
            field,
            field,
            field,
            jax.ShapeDtypeStruct((8, LANES), f32),
        ),
        in_specs=[pl.BlockSpec(memory_space=pl.ANY)] * 3,
        out_specs=[vmem] * 5,
        scratch_shapes=[
            pltpu.VMEM((height, width), f32),
            pltpu.VMEM((height, width), f32),
            pltpu.VMEM((height, width), jnp.int32),
            pltpu.VMEM((rows, subs, LANES), f32),
            pltpu.VMEM((rows, subs, LANES), f32),
            pltpu.VMEM((2, 9, rows, subs, LANES), f32),
            pltpu.VMEM((MICRO_SPELLS, ens, height, subs, LANES), f32),
            pltpu.VMEM((slabs, subs, LANES), f32),
            dma((3,)),
            dma((2, 2)),
            dma((2, 2)),
            dma((MICRO_SPELLS, ens - 1)),
            dma((MICRO_SPELLS, ens - 1)),
            dma((slabs - 1,)),
            dma((slabs - 1,)),
        ],
        compiler_params=pltpu.CompilerParams(collective_id=0, has_side_effects=True),
    )(density0, relax_rate, perturbation)
    projected = fitted + gain[0, 0] * change
    lifted = finals * (projected / last_rho)[None]
    return (lifted[None], projected)


def solution(mesh):
    in_specs = (P("slab", None), P("slab", None), P("ens", "slab", None))
    out_specs = (P("ens", None, "slab", None), P("slab", None))
    return jax.shard_map(
        on_device, mesh=mesh, in_specs=in_specs, out_specs=out_specs, check_vma=False
    )
```

profile of v0, /device:TPU:0, one launch (start us, length us, event | category | flops | bytes accessed | tf_op | source)
XLA Modules:
  0.0 65.8 jit_solution(160654245316917144)
XLA Ops:
  0.6 59.5 %shard_map.50 = (f32[9,24,1024]{2,1,0:T(8,128)}, f32[24,1024]{1,0:T(8,128)}, f32[24,1024]{1,0:T(8,128)}, f32[24,1024]{1,0:T(8,128)}, f32[8,128]{1,0:T(8,128)}) custom-call(f32[24,1024]{1,0:T(8,128)} %density_hbm.1, f32[24,1024]{1,0:T(8,128)} %relax_hbm.1, s32[1,24,1024]{2,1,0:T(8,128)} %pert_hbm.1), custom_call_target="tpu_custom_call" | custom-call | tf_op jit(solution)/shard_map/pallas_call | solution.py:290
  60.2 1.2 %slice.3 = f32[1,1]{1,0:T(1,128)} slice(f32[8,128]{1,0:T(8,128)} %get-tuple-element.9), slice={[0:1], [0:1]} | slice | bytes 8 | tf_op jit(solution)/shard_map/slice | solution.py:320
  61.4 2.3 %fusion = (f32[24,1024]{1,0:T(8,128)S(1)}, f32[24,1024]{1,0:T(8,128)}) fusion(f32[24,1024]{1,0:T(8,128)} %get-tuple-element.11, f32[24,1024]{1,0:T(8,128)} %get-tuple-element.8, f32[24,1024]{1,0:T(8,128)} %get-tuple-element.10, f32[]{:T(128)} %bitcast), kind=kLoop, calls=%fused_computation.2 | loop fusion | flops 73728 | bytes 491524 | tf_op jit(solution)/shard_map/div | solution.py:321
  63.7 2.2 %multiply_bitcast_fusion = f32[1,9,24,1024]{3,2,1,0:T(8,128)} fusion(f32[9,24,1024]{2,1,0:T(8,128)} %get-tuple-element.7, f32[24,1024]{1,0:T(8,128)S(1)} %get-tuple-element.12), kind=kLoop, calls=%fused_computation | loop fusion | flops 221184 | bytes 1867776 | tf_op jit(solution)/shard_map/broadcast_in_dim | solution.py:322
where the time goes:
time: 66.1 us; the launch traced here: 65.8 us
  Pallas kernels  59.5 us (90%)
  other arithmetic  4.47 us (7%)
  local copies, waits for them, and re-layouts  1.18 us (2%)
    pallas_call x1, Pallas kernels, on_device(): pl.pallas_call(functools.partial(kernel, ens, slabs), out_shape=(jax.Shap...  59.5 us
    div x1, other arithmetic, on_device(): lifted = finals * (projected / last_rho)[None]  2.29 us
    broadcast_in_dim x1, other arithmetic, on_device(): return (lifted[None], projected)  2.18 us

commit v1 on v0

--- a/solution.py
+++ b/solution.py
@@ -12,6 +12,9 @@
 TOTAL = MICRO_SPELLS * STEPS
 LANES = 128
 CHUNK = 4
+BIG = 12
+FIRST = 12
+FRONT = 8
 
 row_moves = (0, 0, 1, 0, -1, 1, 1, -1, -1)
 col_moves = (0, 1, 0, -1, 0, 1, -1, -1, 1)
@@ -35,7 +38,7 @@
     return jnp.where(lane == LANES - 1, across, within)
 
 
-def collide(f, relax):
+def collide(f, keep, third, ninth):
     s13, d13 = f[1] + f[3], f[1] - f[3]
     s24, d24 = f[2] + f[4], f[2] - f[4]
     s57, d57 = f[5] + f[7], f[5] - f[7]
@@ -43,18 +46,16 @@
     density = (f[0] + (s13 + s24)) + (s57 + s68)
     mom_row = d24 + (d57 + d68)
     mom_col = d13 + (d57 - d68)
-    inverse = 1.0 / density
+    inverse = 1.5 / density
     vel_row = mom_row * inverse
     vel_col = mom_col * inverse
-    keep = 1.0 - relax
-    third = relax * (1.0 / 3.0)
     third_row = third * mom_row
     third_col = third * mom_col
-    half_rr = third_row * vel_row * 1.5
-    half_cc = third_col * vel_col * 1.5
-    quarter_rc = third_row * vel_col * 0.75
+    half_rr = third_row * vel_row
+    half_cc = third_col * vel_col
+    quarter_rc = (third_row * vel_col) * 0.5
     squares = half_rr + half_cc
-    base = (relax * density) * (1.0 / 9.0) - squares * (1.0 / 3.0)
+    base = ninth * density - squares * (1.0 / 3.0)
     even_col = base + half_cc
     even_row = base + half_rr
     corner = 0.25 * (base + squares)
@@ -79,23 +80,18 @@
 def kernel(
     ens,
     slabs,
-    density_hbm,
-    relax_hbm,
-    pert_hbm,
-    finals,
-    last_rho,
-    change_out,
-    fitted_out,
-    gain_out,
     density_in,
     relax_in,
     pert_in,
+    finals,
+    scale_out,
+    projected_out,
     start,
     relax,
+    coef,
     buf,
     gathered,
     squares,
-    load_sem,
     halo_send,
     halo_recv,
     ens_send,
@@ -119,23 +115,29 @@
             barrier, inc=1, device_id={"slab": lax.rem(me_s + k, slabs)}, device_id_type=MESH
         )
 
-    loads = [
-        pltpu.make_async_copy(relax_hbm, relax_in, load_sem.at[0]),
-        pltpu.make_async_copy(density_hbm, density_in, load_sem.at[1]),
-        pltpu.make_async_copy(pert_hbm.at[0], pert_in, load_sem.at[2]),
-    ]
-    for load in loads:
-        load.start()
     own = pl.ds(TOTAL, height)
-    loads[0].wait()
     for s in range(subs):
         relax[own, s, :] = relax_in[:, s * LANES : (s + 1) * LANES]
-    loads[1].wait()
-    loads[2].wait()
     for s in range(subs):
         cols = slice(s * LANES, (s + 1) * LANES)
-        start[own, s, :] = density_in[:, cols] + shift_amp * pert_in[:, cols].astype(jnp.float32)
-
+        start[own, s, :] = density_in[:, cols] + shift_amp * pert_in[0, :, cols].astype(jnp.float32)
+
+    def first_rows(low, high):
+        def body(c, carry):
+            at = pl.ds(low + c * FIRST, FIRST)
+            fresh = start[at]
+            rate = relax[at]
+            rates = (1.0 - rate, rate * (1.0 / 3.0), rate * (1.0 / 9.0))
+            for n in range(3):
+                coef[n, at] = rates[n]
+            out = collide([weight * fresh for weight in lattice_weights], *rates)
+            for i in range(9):
+                buf[1, i, pl.ds(FRONT + low + c * FIRST, FIRST)] = roll_columns(out[i], col_moves[i])
+            return carry
+
+        lax.fori_loop(0, (high - low) // FIRST, body, 0)
+
+    first_rows(TOTAL, TOTAL + height)
     pl.semaphore_wait(barrier, ens + slabs - 2)
     right = lax.rem(me_s + 1, slabs)
     left = lax.rem(me_s + slabs - 1, slabs)
@@ -157,34 +159,30 @@
     for copy in halos:
         copy.start()
 
-    def first_rows(low, high):
-        def body(c, carry):
-            at = pl.ds(low + c * CHUNK, CHUNK)
-            fresh = start[at]
-            out = collide([weight * fresh for weight in lattice_weights], relax[at])
-            for i in range(9):
-                buf[1, i, at] = roll_columns(out[i], col_moves[i])
-            return carry
-
-        lax.fori_loop(0, (high - low) // CHUNK, body, 0)
-
     def step(k, carry):
         source, dest = lax.rem(k + 1, 2), lax.rem(k, 2)
 
-        def body(c, inner):
-            at = k - 1 + c * CHUNK
-            f = [buf[source, i, pl.ds(at - row_moves[i], CHUNK)] for i in range(9)]
-            out = collide(f, relax[pl.ds(at, CHUNK)])
-            for i in range(9):
-                buf[dest, i, pl.ds(at, CHUNK)] = roll_columns(out[i], col_moves[i])
-            return inner
-
-        lax.fori_loop(0, (rows - 2 * k + 2 + CHUNK - 1) // CHUNK, body, 0)
+        def sweep(low, chunks, size):
+            def body(c, inner):
+                at = FRONT + low + c * size
+                f = [buf[source, i, pl.ds(at - row_moves[i], size)] for i in range(9)]
+                out = collide(f, *(coef[n, pl.ds(at - FRONT, size)] for n in range(3)))
+                for i in range(9):
+                    buf[dest, i, pl.ds(at, size)] = roll_columns(out[i], col_moves[i])
+                return inner
+
+            lax.fori_loop(0, chunks, body, 0)
+
+        count = rows - 2 * k + 2
+        whole = (count + CHUNK // 2) // BIG
+        sweep(k - 1, whole, BIG)
+        rest = jnp.maximum(count - whole * BIG, 0)
+        sweep(k - 1 + whole * BIG, (rest + CHUNK - 1) // CHUNK, CHUNK)
         return carry
 
     def spell_density(spell, parity):
         def body(c, inner):
-            at = TOTAL + c * CHUNK
+            at = FRONT + TOTAL + c * CHUNK
             total = buf[parity, 0, pl.ds(at, CHUNK)]
             for i in range(1, 9):
                 total = total + buf[parity, i, pl.ds(at - row_moves[i], CHUNK)]
@@ -208,7 +206,6 @@
             copy.start()
         return copies
 
-    first_rows(TOTAL, TOTAL + height)
     for copy in halos:
         copy.wait_recv()
     first_rows(0, TOTAL)
@@ -223,8 +220,7 @@
     for s in range(subs):
         cols = slice(s * LANES, (s + 1) * LANES)
         for i in range(9):
-            finals[i, :, cols] = buf[parity, i, pl.ds(TOTAL - row_moves[i], height), s, :]
-        last_rho[:, cols] = gathered[MICRO_SPELLS - 1, me_e, :, s, :]
+            finals[i, :, cols] = buf[parity, i, pl.ds(FRONT + TOTAL - row_moves[i], height), s, :]
 
     for copies in sent:
         for copy in copies:
@@ -260,16 +256,19 @@
         )
     for copy in copies:
         copy.start()
-    for s in range(subs):
-        cols = slice(s * LANES, (s + 1) * LANES)
-        change_out[:, cols] = start[pl.ds(0, height), s, :]
-        fitted_out[:, cols] = relax[pl.ds(0, height), s, :]
     for copy in copies:
         copy.wait_recv()
     total = jnp.sum(jnp.sum(squares[...], axis=0), axis=(0, 1), keepdims=True)
     mean_square = total * (1.0 / (height * width * slabs))
-    gain = step_cap / jnp.sqrt(mean_square + 1e-06)
-    gain_out[...] = jnp.broadcast_to(gain, gain_out.shape)
+    gain = (step_cap / jnp.sqrt(mean_square + 1e-06))[None]
+    field = pl.ds(0, height)
+    projected = relax[field] + gain * start[field]
+    start[field] = projected
+    relax[field] = projected / gathered[MICRO_SPELLS - 1, me_e]
+    for s in range(subs):
+        cols = slice(s * LANES, (s + 1) * LANES)
+        projected_out[:, cols] = start[field, s, :]
+        scale_out[:, cols] = relax[field, s, :]
 
     for group in [halos, copies] + sent:
         for copy in group:
@@ -280,34 +279,30 @@
     height, width = density0.shape
     ens, slabs = lax.axis_size("ens"), lax.axis_size("slab")
     assert perturbation.shape[0] == 1 and height >= TOTAL and width % LANES == 0
-    assert height % CHUNK == 0 and TOTAL % CHUNK == 0
+    assert height % CHUNK == 0 and CHUNK <= FRONT
+    assert height % FIRST == 0 and TOTAL % FIRST == 0
     subs = width // LANES
-    rows = height + 2 * TOTAL + CHUNK
+    rows = height + 2 * TOTAL + max(CHUNK, FIRST)
     f32 = jnp.float32
     field = jax.ShapeDtypeStruct((height, width), f32)
     vmem = pl.BlockSpec(memory_space=pltpu.VMEM)
     dma = pltpu.SemaphoreType.DMA
-    finals, last_rho, change, fitted, gain = pl.pallas_call(
+    finals, scale, projected = pl.pallas_call(
         functools.partial(kernel, ens, slabs),
         out_shape=(
             jax.ShapeDtypeStruct((9, height, width), f32),
             field,
             field,
-            field,
-            jax.ShapeDtypeStruct((8, LANES), f32),
         ),
-        in_specs=[pl.BlockSpec(memory_space=pl.ANY)] * 3,
-        out_specs=[vmem] * 5,
+        in_specs=[vmem] * 3,
+        out_specs=[vmem] * 3,
         scratch_shapes=[
-            pltpu.VMEM((height, width), f32),
-            pltpu.VMEM((height, width), f32),
-            pltpu.VMEM((height, width), jnp.int32),
             pltpu.VMEM((rows, subs, LANES), f32),
             pltpu.VMEM((rows, subs, LANES), f32),
-            pltpu.VMEM((2, 9, rows, subs, LANES), f32),
+            pltpu.VMEM((3, rows, subs, LANES), f32),
+            pltpu.VMEM((2, 9, rows + FRONT, subs, LANES), f32),
             pltpu.VMEM((MICRO_SPELLS, ens, height, subs, LANES), f32),
             pltpu.VMEM((slabs, subs, LANES), f32),
-            dma((3,)),
             dma((2, 2)),
             dma((2, 2)),
             dma((MICRO_SPELLS, ens - 1)),
@@ -315,10 +310,11 @@
             dma((slabs - 1,)),
             dma((slabs - 1,)),
         ],
-        compiler_params=pltpu.CompilerParams(collective_id=0, has_side_effects=True),
+        compiler_params=pltpu.CompilerParams(
+            collective_id=0, has_side_effects=True, vmem_limit_bytes=24 << 20
+        ),
     )(density0, relax_rate, perturbation)
-    projected = fitted + gain[0, 0] * change
-    lifted = finals * (projected / last_rho)[None]
+    lifted = finals * scale[None]
     return (lifted[None], projected)
 
 

time: 66.1 us -> 50.7 us (0.77)
  Pallas kernels: 59.5 us -> 45.5 us
  other arithmetic: 4.47 us -> 1.01 us
  local copies, waits for them, and re-layouts: 1.18 us -> 3.31 us
    pallas_call x1, Pallas kernels: 59.5 us -> 45.5 us  [on_device(): pl.pallas_call(functools.partial(kernel, ens, slabs), out_shape=(jax.Shap...]
    unnamed x0 -> x7, local copies, waits for them, and re-layouts: none -> 3.31 us
    div x1 -> x0, other arithmetic: 2.29 us -> none  [on_device(): lifted = finals * (projected / last_rho)[None]]
    slice x1 -> x0, local copies, waits for them, and re-layouts: 1.18 us -> none  [on_device(): projected = fitted + gain[0, 0] * change]
    broadcast_in_dim x1, other arithmetic: 2.18 us -> 1.01 us  [on_device(): return (lifted[None], projected)]
where the time goes in v1:
time: 50.7 us; the launch traced here: 50.5 us
  Pallas kernels  45.5 us (90%)
  local copies, waits for them, and re-layouts  3.31 us (7%)
  other arithmetic  1.01 us (2%)
  between operations  0.65 us (1%)
    pallas_call x1, Pallas kernels, on_device(): pl.pallas_call(functools.partial(kernel, ens, slabs), out_shape=(jax.Shap...  45.5 us
    unnamed x7, local copies, waits for them, and re-layouts  3.31 us
    broadcast_in_dim x1, other arithmetic, on_device(): return (lifted[None], projected)  1.01 us

profile of v1, /device:TPU:0, one launch (start us, length us, event | category | flops | bytes accessed | tf_op | source)
XLA Modules:
  0.0 50.5 jit_solution(17582079595909917068)
XLA Ops:
  0.6 0.0 copy-start
  0.6 0.9 %copy-done = f32[24,1024]{1,0:T(8,128)S(1)} copy-done((f32[24,1024]{1,0:T(8,128)S(1)}, f32[24,1024]{1,0:T(8,128)}, u32[]{:S(2)}) %copy-start) | copy-done | bytes 98328
  1.5 0.0 copy-start.1
  1.5 0.9 %copy-done.1 = f32[24,1024]{1,0:T(8,128)S(1)} copy-done((f32[24,1024]{1,0:T(8,128)S(1)}, f32[24,1024]{1,0:T(8,128)}, u32[]{:S(2)}) %copy-start.1) | copy-done | bytes 98328
  2.4 0.0 copy-start.2
  2.4 0.9 %copy-done.2 = s32[1,24,1024]{2,1,0:T(8,128)S(1)} copy-done((s32[1,24,1024]{2,1,0:T(8,128)S(1)}, s32[1,24,1024]{2,1,0:T(8,128)}, u32[]{:S(2)}) %copy-start.2) | copy-done | bytes 98328
  3.3 45.5 %shard_map.50 = (f32[9,24,1024]{2,1,0:T(8,128)S(1)}, f32[24,1024]{1,0:T(8,128)S(1)}, f32[24,1024]{1,0:T(8,128)S(1)}) custom-call(f32[24,1024]{1,0:T(8,128)S(1)} %copy-done, f32[24,1024]{1,0:T(8,128)S(1)} %copy-done.1, s32[1,24,1024]{2,1,0:T(8,128)S(1)} %copy-done.2), custom_call_target="tpu_custom_call" | custom-call | tf_op jit(solution)/shard_map/pallas_call | solution.py:290
  48.8 1.0 %multiply_bitcast_fusion = f32[1,9,24,1024]{3,2,1,0:T(8,128)} fusion(f32[9,24,1024]{2,1,0:T(8,128)S(1)} %get-tuple-element.5, f32[24,1024]{1,0:T(8,128)S(1)} %get-tuple-element.6), kind=kLoop, calls=%fused_computation | loop fusion | flops 221184 | bytes 1867776 | tf_op jit(solution)/shard_map/broadcast_in_dim | solution.py:318
  49.8 0.6 %copy.6 = f32[24,1024]{1,0:T(8,128)} copy(f32[24,1024]{1,0:T(8,128)S(1)} %get-tuple-element.11) | data formatting | bytes 196608
Async XLA Ops:
  0.6 0.9 %copy-start = (f32[24,1024]{1,0:T(8,128)S(1)}, f32[24,1024]{1,0:T(8,128)}, u32[]{:S(2)}) copy-start(f32[24,1024]{1,0:T(8,128)} %density_in.1) | copy-start | bytes 294916
  1.5 0.9 %copy-start.1 = (f32[24,1024]{1,0:T(8,128)S(1)}, f32[24,1024]{1,0:T(8,128)}, u32[]{:S(2)}) copy-start(f32[24,1024]{1,0:T(8,128)} %relax_in.1) | copy-start | bytes 294916
  2.4 0.9 %copy-start.2 = (s32[1,24,1024]{2,1,0:T(8,128)S(1)}, s32[1,24,1024]{2,1,0:T(8,128)}, u32[]{:S(2)}) copy-start(s32[1,24,1024]{2,1,0:T(8,128)} %pert_in.1) | copy-start | bytes 294916
